TPU v7x, 8 devices: a whole 2x2x1 slice. The times are simulated.
8 devices in a mesh: bx: 2 (over z, y), sq: 4 (over x, core).
Axes of the slice: x: 2, y: 2, z: 1, core: 2. Of those that a mesh axis runs over, the one named last changes fastest.
Arguments:
- hidden: bfloat16 [128, 2048], P('bx'), parts along dimension 0
- w_query: bfloat16 [2048, 2048], P(None, 'sq')
- w_key: bfloat16 [2048, 128], replicated
- w_value: bfloat16 [2048, 128], replicated
- w_out: bfloat16 [2048, 2048], P('sq')
- k_cache: bfloat16 [128, 8192, 128], P('bx', 'sq'), parts along dimension 0
- v_cache: bfloat16 [128, 8192, 128], P('bx', 'sq'), parts along dimension 0
- lengths: int32 [128], P('bx'), parts along dimension 0
Outputs:
- output 1: bfloat16 [128, 2048], P('bx', 'sq'), parts along dimension 0
- output 2: bfloat16 [128, 128], P('bx'), parts along dimension 0
- output 3: bfloat16 [128, 128], P('bx'), parts along dimension 0
There are 2 independent parts. A program takes and returns all parts, laid end to end along the dimension named above; an argument that names none is the same for every part.
All inputs are finite; a program needn't handle non-finite values.
Results may differ from a plain program's by a relative error of at most 0.00560568.
Values sent between devices are 32-bit elements.
A program may use at most 1 GiB of HBM per device.

v0:
```python
import math
import jax
import jax.numpy as jnp
from jax import lax
from jax.experimental import pallas as pl
from jax.experimental.pallas import tpu as pltpu
from jax.sharding import PartitionSpec as P

ROPE_BASE = 10000.0
GROUP = 8
RING = 3
CHUNK = 512
PIECE = 4
MASKED = -3e38
MESH = pl.DeviceIdType.MESH
Y_BATCHES = {3: (0, 2), 4: (2, 1)}


def make_kernel(rows, embed, seq, heads_local, hd):
    n_groups = rows // GROUP
    n_heads = 4 * heads_local
    assert n_heads * GROUP == hd and hd == 128
    q_cols = heads_local * hd
    last = n_groups - 1
    exp_c = hd ** -0.5 * math.log2(math.e)
    n_pieces = GROUP // PIECE
    piece_rows = heads_local * PIECE
    half = hd // 2
    freqs = [ROPE_BASE ** (-2.0 * i / hd) for i in range(half)]
    prow = heads_local * GROUP

    def kernel(hid_hbm, wq_hbm, wk_hbm, wv_hbm, wo_hbm, k_hbm, v_hbm, len_hbm,
               y_out, kn_out, vn_out,
               hid, wq, wkv, wo, lens_s, kb, vb, qown, qrec, qmat, qblk, k_turn, sbuf, oacc, mrow,
               vnf, snew, wts, psend, prec, tsend, trec, attn, ysend,
               in_sem, ksem, vsem, tsem, qs_sem, qr_sem, ps_sem, pr_sem, ts_sem, tr_sem, ys_sem, yr_sem):
        bx = lax.axis_index('bx')
        me = lax.axis_index('sq')
        chip, core = me // 2, me % 2
        peers = [chip * 2 + (1 - core), (1 - chip) * 2 + core, (1 - chip) * 2 + (1 - core)]
        far_first = (1, 2, 0)
        base = me * seq

        def cp(src, dst, sem):
            return pltpu.make_async_copy(src, dst, sem)

        def k_copy(g):
            return cp(k_hbm.at[pl.ds(g * GROUP, GROUP)], kb.at[g % RING], ksem.at[g % RING])

        def v_copy(g):
            return cp(v_hbm.at[pl.ds(g * GROUP, GROUP)], vb.at[g % RING], vsem.at[g % RING])

        def v_tail(c):
            r0 = last * GROUP + c * PIECE
            return cp(v_hbm.at[r0:r0 + PIECE], vb.at[last % RING, c * PIECE:(c + 1) * PIECE], tsem.at[c])

        ins = [cp(len_hbm, lens_s, in_sem.at[0]), cp(hid_hbm, hid, in_sem.at[1]), cp(wq_hbm, wq, in_sem.at[2]),
               cp(wk_hbm, wkv.at[0], in_sem.at[3]), cp(wv_hbm, wkv.at[1], in_sem.at[4]), cp(wo_hbm, wo, in_sem.at[5])]
        for c in ins[:5]:
            c.start()
        k_copy(0).start()
        k_copy(1).start()
        v_copy(0).start()

        barrier = pltpu.get_barrier_semaphore()
        for p in peers:
            pl.semaphore_signal(barrier, inc=1, device_id=(bx, p), device_id_type=MESH)

        k_copy(2).start()
        v_copy(1).start()
        ins[5].start()

        lane = lax.broadcasted_iota(jnp.int32, (1, hd), 1)
        lane_i = lane % half
        freq = jnp.zeros((1, hd), jnp.float32)
        for i in range(half):
            freq = jnp.where(lane_i == i, jnp.float32(freqs[i]), freq)
        ins[0].wait()
        sub = lax.broadcasted_iota(jnp.int32, (GROUP, 1), 0)
        pos_rows = []
        for g in range(n_groups):
            t = jnp.zeros((GROUP, 1), jnp.int32)
            for r in range(GROUP):
                t = jnp.where(sub == r, lens_s[g * GROUP + r], t)
            pos_rows.append(t)
        t_col = jnp.concatenate(pos_rows, axis=0).astype(jnp.float32)
        ang = t_col * freq
        cos_t = jnp.cos(ang)
        sin_t = jnp.where(lane < half, -1.0, 1.0) * jnp.sin(ang)

        def rope(x):
            return x * cos_t + pltpu.roll(x, half, 1) * sin_t

        ins[1].wait()
        ins[2].wait()
        qp = jnp.dot(hid[...], wq[...], preferred_element_type=jnp.float32)
        for h in range(heads_local):
            cs = slice(h * hd, (h + 1) * hd)
            q_h = rope(qp[:, cs]).astype(jnp.bfloat16).astype(jnp.float32)
            qown[:, :, cs] = q_h.reshape(n_groups, GROUP, hd)
        pl.semaphore_wait(barrier, 3)

        def q_copy(g, d):
            return pltpu.make_async_remote_copy(
                src_ref=qown.at[g], dst_ref=qrec.at[g, d], send_sem=qs_sem.at[d],
                recv_sem=qr_sem.at[g], device_id=(bx, peers[d]), device_id_type=MESH)

        for g in range(n_groups):
            for d in far_first:
                q_copy(g, d).start()

        ins[3].wait()
        ins[4].wait()
        kn = rope(jnp.dot(hid[...], wkv[0], preferred_element_type=jnp.float32)).astype(jnp.bfloat16)
        vn = jnp.dot(hid[...], wkv[1], preferred_element_type=jnp.float32).astype(jnp.bfloat16)
        kn_out[...] = kn
        vn_out[...] = vn
        knf = kn.astype(jnp.float32)
        vnf[...] = vn.astype(jnp.float32)
        for h in range(heads_local):
            q_h = qown[:, :, h * hd:(h + 1) * hd].reshape(rows, hd)
            s_h = jnp.sum(q_h * knf, axis=1, keepdims=True)
            snew[h] = jnp.broadcast_to(s_h, (rows, hd))

        def per_row(g, vals):
            return jnp.concatenate([jnp.full((n_heads, 1), vals(g * GROUP + r), jnp.int32) for r in range(GROUP)], axis=0)

        def lens_col(g):
            return per_row(g, lambda b: lens_s[b])

        qblk[...] = jnp.zeros_like(qblk)

        def q_wait(g):
            pltpu.make_async_copy(qrec.at[g], qrec.at[g], qr_sem.at[g]).wait()

        def build_q(g):
            for s in range(4):
                for h in range(heads_local):
                    cs = slice(h * hd, (h + 1) * hd)
                    blk = qown[g, :, cs] if s == 3 else qrec[g, s, :, cs]
                    qmat[pl.ds(s * heads_local + h, GROUP, stride=n_heads), :] = blk
            for r in range(GROUP):
                rs = slice(r * n_heads, (r + 1) * n_heads)
                qblk[rs, (r % 2) * hd:(r % 2 + 1) * hd] = qmat[rs, :].astype(jnp.bfloat16)

        def fold(x, op):
            out = x[:, :hd]
            for i in range(1, x.shape[1] // hd):
                out = op(out, x[:, i * hd:(i + 1) * hd])
            return out

        def score_tile(g, t, lo, ln, m, turn=True):
            rs = slice(2 * t * n_heads, (2 * t + 2) * n_heads)
            kc = jnp.concatenate([kb[g % RING, 2 * t + i, lo:lo + CHUNK, :] for i in range(2)], axis=1)
            if turn:
                k_turn[t % 2] = kc.T
                kt = k_turn[t % 2]
            else:
                kt = kc.T
            s = jnp.dot(qblk[rs, :], kt, preferred_element_type=jnp.float32)
            pos = lax.broadcasted_iota(jnp.int32, (1, CHUNK), 1) + (base + lo)
            s = jnp.where(pos < ln[rs, :], s, MASKED)
            sbuf[g % 2, rs, lo:lo + CHUNK] = s
            return jnp.maximum(m, fold(s, jnp.maximum))

        n_pairs = GROUP // 2
        pair_rows = 2 * n_heads

        def no_max():
            return [jnp.full((pair_rows, hd), MASKED, jnp.float32) for _ in range(n_pairs)]

        def scores(g, ln):
            ms = no_max()
            for lo in range(0, seq, CHUNK):
                ms = [score_tile(g, t, lo, ln, ms[t], t < n_pairs - 1) for t in range(n_pairs)]
            return ms

        def weights(g, lo, size, mu):
            w = jnp.exp2((sbuf[g % 2, :, lo:lo + size] - mu) * exp_c)
            return w.astype(jnp.bfloat16), fold(w, jnp.add)

        def weighted(g, r, wt, lo, size):
            vc = jnp.concatenate([vb[g % RING, r + i, lo:lo + size, :] for i in range(2)], axis=1)
            o = jnp.dot(wt, vc, preferred_element_type=jnp.float32)
            return jnp.concatenate([o[:n_heads, :hd], o[n_heads:, hd:]], axis=0)

        def attend(g, mu, ln):
            outs = [None] * n_pairs
            ms = no_max()
            l = jnp.zeros((hd, hd), jnp.float32)
            for lo in range(0, seq, CHUNK):
                wt, part = weights(g, lo, CHUNK, mu)
                l = l + part
                for t in range(n_pairs):
                    if ln is not None:
                        ms[t] = score_tile(g + 1, t, lo, ln, ms[t])
                    o = weighted(g, 2 * t, wt[t * pair_rows:(t + 1) * pair_rows, :], lo, CHUNK)
                    outs[t] = o if outs[t] is None else outs[t] + o
            for t in range(n_pairs):
                oacc[t * pair_rows:(t + 1) * pair_rows, :] = outs[t]
            return ms, l

        def keep_max(g, ms):
            m = jnp.concatenate(ms, axis=0)
            mrow[g % 2] = jnp.broadcast_to(jnp.max(m, axis=1, keepdims=True), (hd, hd))

        def stat_rows(g, l):
            l_col = jnp.sum(l, axis=1, keepdims=True)
            return jnp.where(lane == 0, mrow[g % 2], jnp.where(lane == 1, l_col, 0.0)).T[:8, :]

        def p_copy(g, d):
            return pltpu.make_async_remote_copy(
                src_ref=psend.at[d, g], dst_ref=prec.at[g, d], send_sem=ps_sem.at[d],
                recv_sem=pr_sem.at[g], device_id=(bx, peers[d]), device_id_type=MESH)

        def send_part(g, l):
            for h in range(n_heads):
                k, hh = h // heads_local, h % heads_local
                psend[k, g, hh * GROUP:(hh + 1) * GROUP, :] = oacc[pl.ds(h, GROUP, stride=n_heads), :]
            ml = stat_rows(g, l)
            for k in range(4):
                psend[k, g, prow:prow + 8, :] = ml
            for d in far_first:
                p_copy(g, d).start()

        def t_copy(c, d):
            return pltpu.make_async_remote_copy(
                src_ref=tsend.at[d, c], dst_ref=trec.at[c, d], send_sem=ts_sem.at[d],
                recv_sem=tr_sem.at[c], device_id=(bx, peers[d]), device_id_type=MESH)

        def send_piece(c, ml):
            for h in range(n_heads):
                k, hh = h // heads_local, h % heads_local
                tsend[k, c, hh * PIECE:(hh + 1) * PIECE, :] = (
                    oacc[pl.ds(c * PIECE * n_heads + h, PIECE, stride=n_heads), :])
            for k in range(4):
                tsend[k, c, piece_rows:piece_rows + 8, :] = ml
            for d in far_first:
                t_copy(c, d).start()

        def picks(nr, r0):
            row = lax.broadcasted_iota(jnp.int32, (heads_local * nr, hd), 0)
            at = (r0 + row % nr) * n_heads + row // nr
            lane_p = lax.broadcasted_iota(jnp.int32, (heads_local * nr, hd), 1)
            return [lane_p == at + d * heads_local for d in range(4)]

        def combine_rows(parts, row0, nr, picked):
            n = heads_local * nr
            rs = slice(row0, row0 + nr)

            def to_col(d, row):
                return jnp.sum(jnp.where(picked[d], row, 0.0), axis=1, keepdims=True)

            s_new = jnp.concatenate([snew[h, rs, :] for h in range(heads_local)], axis=0)
            ms = [to_col(d, p[n:n + 1, :]) for d, p in enumerate(parts)]
            ls = [to_col(d, p[n + 1:n + 2, :]) for d, p in enumerate(parts)]
            top = s_new
            for m in ms:
                top = jnp.maximum(top, m)
            f_new = jnp.exp2((s_new - top) * exp_c)
            den = f_new
            num = f_new * jnp.concatenate([vnf[rs, :]] * heads_local, axis=0)
            for p, m, l in zip(parts, ms, ls):
                f = jnp.exp2((m - top) * exp_c)
                den = den + f * l
                num = num + f * p[:n, :]
            o = num / den
            for h in range(heads_local):
                attn[rs, h * hd:(h + 1) * hd] = o[h * nr:(h + 1) * nr, :]

        def combine(g):
            parts = [prec[g, d] for d in range(3)] + [psend[3, g]]
            combine_rows(parts, g * GROUP, GROUP, picks(GROUP, 0))

        def combine_piece(c):
            pltpu.make_async_copy(trec.at[c], trec.at[c], tr_sem.at[c]).wait()
            parts = [trec[c, d] for d in range(3)] + [tsend[3, c]]
            combine_rows(parts, last * GROUP + c * PIECE, PIECE, picks(PIECE, c * PIECE))

        def p_wait(g):
            pltpu.make_async_copy(prec.at[g], prec.at[g], pr_sem.at[g]).wait()

        y_batches = []

        def y_copy(b, g0, ng, d):
            sl = pl.ds(g0 * GROUP, ng * GROUP)
            return pltpu.make_async_remote_copy(
                src_ref=ysend.at[peers[d], sl], dst_ref=y_out.at[d, sl], send_sem=ys_sem.at[d],
                recv_sem=yr_sem.at[b], device_id=(bx, peers[d]), device_id_type=MESH)

        def project(g0, ng):
            b = len(y_batches)
            y_batches.append((b, g0, ng))
            sl = slice(g0 * GROUP, (g0 + ng) * GROUP)
            yp = jnp.dot(attn[sl, :].astype(jnp.bfloat16), wo[...], preferred_element_type=jnp.float32)
            for k in range(4):
                ysend[k, sl, :] = yp[:, k * q_cols:(k + 1) * q_cols]
            for d in far_first:
                y_copy(b, g0, ng, d).start()
            y_out[3, sl, :] = ysend[me, sl, :]

        def finish(b, g0, ng):
            sl = pl.ds(g0 * GROUP, ng * GROUP)
            pltpu.make_async_copy(y_out.at[0:3, sl], y_out.at[0:3, sl], yr_sem.at[b]).wait()

        q_wait(0)
        build_q(0)
        k_copy(0).wait()
        keep_max(0, scores(0, lens_col(0)))

        def shift(g):
            return jnp.where(lens_col(g) > base, mrow[g % 2, :, 0:1], 0.0)

        for g in range(last - 1):
            if g + 3 < n_groups:
                k_copy(g + 3).start()
            if g + 2 < last:
                v_copy(g + 2).start()
            if g + 2 == last:
                for c in range(n_pieces):
                    v_tail(c).start()
            q_wait(g + 1)
            if g >= 2:
                p_wait(g - 2)
            if g == 3:
                ins[5].wait()
            k_copy(g + 1).wait()
            v_copy(g).wait()
            build_q(g + 1)
            ms, l = attend(g, shift(g), lens_col(g + 1))
            keep_max(g + 1, ms)
            send_part(g, l)
            if g >= 2:
                combine(g - 2)
            if g in Y_BATCHES:
                project(*Y_BATCHES[g])

        pre = last - 1
        q_wait(last)
        k_copy(last).wait()
        build_q(last)
        keep_max(last, scores(last, lens_col(last)))
        v_copy(pre).wait()
        mu = shift(last)
        pre_l = attend(pre, shift(pre), None)[1]
        l = jnp.zeros((hd, hd), jnp.float32)
        for lo in range(0, seq, CHUNK):
            wt, part = weights(last, lo, CHUNK, mu)
            wts[:, lo:lo + CHUNK] = wt
            l = l + part
        ml = stat_rows(last, l)
        send_part(pre, pre_l)
        for c in range(n_pieces):
            v_tail(c).wait()
            for r in range(c * PIECE, (c + 1) * PIECE, 2):
                rs = slice(r * n_heads, (r + 2) * n_heads)
                oacc[rs, :] = weighted(last, r, wts[rs, :], 0, seq)
            send_piece(c, ml)
        done = max(g0 + ng for g0, ng in Y_BATCHES.values())
        for g in (pre - 2, pre - 1):
            p_wait(g)
            combine(g)
        project(done, pre - done)
        p_wait(pre)
        combine(pre)
        project(pre, 1)
        for c in range(n_pieces):
            combine_piece(c)
        project(last, 1)
        for b in y_batches:
            finish(*b)
        for d in range(3):
            pltpu.make_async_copy(qown, qown, qs_sem.at[d]).wait()
            pltpu.make_async_copy(psend.at[d], psend.at[d], ps_sem.at[d]).wait()
            pltpu.make_async_copy(tsend.at[d], tsend.at[d], ts_sem.at[d]).wait()
            pltpu.make_async_copy(ysend.at[d], ysend.at[d], ys_sem.at[d]).wait()

    f32, bf16 = jnp.float32, jnp.bfloat16
    dma = pltpu.SemaphoreType.DMA
    n_b = len(Y_BATCHES) + 3
    scratch = [
        pltpu.VMEM((rows, embed), bf16), pltpu.VMEM((embed, q_cols), bf16), pltpu.VMEM((2, embed, hd), bf16),
        pltpu.VMEM((q_cols, embed), bf16), pltpu.SMEM((rows,), jnp.int32),
        pltpu.VMEM((RING, GROUP, seq, hd), bf16), pltpu.VMEM((RING, GROUP, seq, hd), bf16),
        pltpu.VMEM((n_groups, GROUP, q_cols), f32), pltpu.VMEM((n_groups, 3, GROUP, q_cols), f32),
        pltpu.VMEM((hd, hd), f32), pltpu.VMEM((hd, 2 * hd), bf16), pltpu.VMEM((2, 2 * hd, CHUNK), bf16),
        pltpu.VMEM((2, hd, seq), f32), pltpu.VMEM((hd, hd), f32), pltpu.VMEM((2, hd, hd), f32),
        pltpu.VMEM((rows, hd), f32),
        pltpu.VMEM((heads_local, rows, hd), f32),
        pltpu.VMEM((hd, seq), bf16),
        pltpu.VMEM((4, last, prow + 8, hd), f32), pltpu.VMEM((last, 3, prow + 8, hd), f32),
        pltpu.VMEM((4, n_pieces, piece_rows + 8, hd), f32), pltpu.VMEM((n_pieces, 3, piece_rows + 8, hd), f32),
        pltpu.VMEM((rows, q_cols), f32), pltpu.VMEM((4, rows, q_cols), f32),
        dma((6,)), dma((RING,)), dma((RING,)), dma((n_pieces,)), dma((3,)), dma((n_groups,)),
        dma((3,)), dma((last,)), dma((3,)), dma((n_pieces,)), dma((3,)), dma((n_b,)),
    ]
    return kernel, scratch


def store_kernel(y_ref, k_ref, v_ref, yo_ref, ko_ref, vo_ref, y16, sem):
    y16[...] = (y_ref[3] + y_ref[0] + y_ref[1] + y_ref[2]).astype(y16.dtype)
    writes = [pltpu.make_async_copy(a, b, sem.at[i])
              for i, (a, b) in enumerate(((y16, yo_ref), (k_ref, ko_ref), (v_ref, vo_ref)))]
    for w in writes:
        w.start()
    for w in writes:
        w.wait()


def solution(mesh):
    def local_step(hidden, w_query, w_key, w_value, w_out, k_cache, v_cache, lengths):
        rows, embed = hidden.shape
        hd = w_key.shape[1]
        seq = k_cache.shape[1]
        heads_local = w_query.shape[1] // hd
        q_cols = heads_local * hd
        kernel, scratch = make_kernel(rows, embed, seq, heads_local, hd)
        any_spec = pl.BlockSpec(memory_space=pl.ANY)
        vmem_spec = pl.BlockSpec(memory_space=pltpu.VMEM)
        outs = (jax.ShapeDtypeStruct((rows, q_cols), jnp.bfloat16),
                jax.ShapeDtypeStruct((rows, hd), jnp.bfloat16),
                jax.ShapeDtypeStruct((rows, hd), jnp.bfloat16))
        raw = pl.pallas_call(
            kernel,
            out_shape=tuple(pltpu.VMEM(sh, dt) for sh, dt in (((4, rows, q_cols), jnp.float32),
                                                              ((rows, hd), jnp.bfloat16), ((rows, hd), jnp.bfloat16))),
            in_specs=[any_spec] * 8,
            out_specs=(vmem_spec,) * 3,
            scratch_shapes=scratch,
            compiler_params=pltpu.CompilerParams(
                collective_id=0, has_side_effects=True, vmem_limit_bytes=66300000),
            name="mqa_decode",
        )(hidden, w_query, w_key, w_value, w_out, k_cache, v_cache, lengths)
        return pl.pallas_call(
            store_kernel,
            out_shape=outs,
            in_specs=[vmem_spec] * 3,
            out_specs=(any_spec,) * 3,
            scratch_shapes=[pltpu.VMEM(outs[0].shape, outs[0].dtype), pltpu.SemaphoreType.DMA((3,))],
            name="store_outputs",
        )(*[pltpu.with_memory_space_constraint(r, pltpu.VMEM) for r in raw])

    return jax.shard_map(
        local_step,
        mesh=mesh,
        in_specs=(P('bx', None), P(None, 'sq'), P(None, None), P(None, None), P('sq', None),
                  P('bx', 'sq', None), P('bx', 'sq', None), P('bx')),
        out_specs=(P('bx', 'sq'), P('bx', None), P('bx', None)),
        check_vma=False,
    )
```

profile of v0, /device:TPU:0, one launch (start us, length us, event | category | flops | bytes accessed | tf_op | source)
XLA Modules:
  0.0 33.6 jit_solution(6725851346602339181)
XLA Ops:
  0.6 32.1 %mqa_decode.1 = (f32[4,64,512]{2,1,0:T(8,128)S(1)}, bf16[64,128]{1,0:T(8,128)(2,1)S(1)}, bf16[64,128]{1,0:T(8,128)(2,1)S(1)}) custom-call(bf16[64,2048]{1,0:T(8,128)(2,1)} %hid_hbm.1, bf16[2048,512]{1,0:T(8,128)(2,1)} %wq_hbm.1, bf16[2048,128]{1,0:T(8,128)(2,1)} %wk_hbm.1, bf16[2048,128]{1,0:T(8,128)(2,1)} %wv_hbm.1, bf16[512,2048]{1,0:T(8,128)(2,1)} %wo_hbm.1, ...), custom_call_target="tpu_custom_call" | custom-call | tf_op jit(solution)/shard_map/mqa_decode/pallas_call | solution.py:423
  32.7 0.7 %store_outputs.1 = (bf16[64,512]{1,0:T(8,128)(2,1)}, bf16[64,128]{1,0:T(8,128)(2,1)}, bf16[64,128]{1,0:T(8,128)(2,1)}) custom-call(f32[4,64,512]{2,1,0:T(8,128)S(1)} %get-tuple-element.6.y_ref, bf16[64,128]{1,0:T(8,128)(2,1)S(1)} %get-tuple-element.7.k_ref, bf16[64,128]{1,0:T(8,128)(2,1)S(1)} %get-tuple-element.8.v_ref), custom_call_target="tpu_custom_call" | custom-call | tf_op jit(solution)/shard_map/store_outputs/pallas_call | solution.py:434
where the time goes:
time: 33.7 us; the launch traced here: 33.6 us
  Pallas kernels  32.8 us (97%)
  between operations  0.8 us (2%)
    pallas_call x1, Pallas kernels, local_step(): pl.pallas_call(kernel, out_shape=tuple((pltpu.VMEM(sh, dt) for sh, dt in...  32.1 us
    pallas_call x1, Pallas kernels, local_step(): pl.pallas_call(store_kernel, out_shape=outs, in_specs=[vmem_spec] * 3, ou...  0.69 us

commit v1 on v0

--- a/solution.py
+++ b/solution.py
@@ -30,10 +30,10 @@
     prow = heads_local * GROUP
 
     def kernel(hid_hbm, wq_hbm, wk_hbm, wv_hbm, wo_hbm, k_hbm, v_hbm, len_hbm,
-               y_out, kn_out, vn_out,
+               y_out, yl_out, kn_out, vn_out,
                hid, wq, wkv, wo, lens_s, kb, vb, qown, qrec, qmat, qblk, k_turn, sbuf, oacc, mrow,
-               vnf, snew, wts, psend, prec, tsend, trec, attn, ysend,
-               in_sem, ksem, vsem, tsem, qs_sem, qr_sem, ps_sem, pr_sem, ts_sem, tr_sem, ys_sem, yr_sem):
+               vnf, snew, wts, psend, prec, tsend, trec, attn, ysend, ylsend,
+               in_sem, ksem, vsem, tsem, qs_sem, qr_sem, ps_sem, pr_sem, ts_sem, tr_sem, yls_sem, ylr_sem, ys_sem, yr_sem):
         bx = lax.axis_index('bx')
         me = lax.axis_index('sq')
         chip, core = me // 2, me % 2
@@ -224,8 +224,9 @@
                 p_copy(g, d).start()
 
         def t_copy(c, d):
+            n = piece_rows + (8 if c == 0 else 0)
             return pltpu.make_async_remote_copy(
-                src_ref=tsend.at[d, c], dst_ref=trec.at[c, d], send_sem=ts_sem.at[d],
+                src_ref=tsend.at[d, c, 0:n], dst_ref=trec.at[c, d, 0:n], send_sem=ts_sem.at[d, c],
                 recv_sem=tr_sem.at[c], device_id=(bx, peers[d]), device_id_type=MESH)
 
         def send_piece(c, ml):
@@ -233,8 +234,9 @@
                 k, hh = h // heads_local, h % heads_local
                 tsend[k, c, hh * PIECE:(hh + 1) * PIECE, :] = (
                     oacc[pl.ds(c * PIECE * n_heads + h, PIECE, stride=n_heads), :])
-            for k in range(4):
-                tsend[k, c, piece_rows:piece_rows + 8, :] = ml
+            if c == 0:
+                for k in range(4):
+                    tsend[k, c, piece_rows:piece_rows + 8, :] = ml
             for d in far_first:
                 t_copy(c, d).start()
 
@@ -273,8 +275,11 @@
             combine_rows(parts, g * GROUP, GROUP, picks(GROUP, 0))
 
         def combine_piece(c):
-            pltpu.make_async_copy(trec.at[c], trec.at[c], tr_sem.at[c]).wait()
-            parts = [trec[c, d] for d in range(3)] + [tsend[3, c]]
+            n = piece_rows + (8 if c == 0 else 0)
+            pltpu.make_async_copy(trec.at[c, :, 0:n], trec.at[c, :, 0:n], tr_sem.at[c]).wait()
+            stats = slice(piece_rows, piece_rows + 8)
+            parts = [jnp.concatenate([trec[c, d, 0:piece_rows, :], trec[0, d, stats, :]], axis=0) for d in range(3)]
+            parts.append(jnp.concatenate([tsend[3, c, 0:piece_rows, :], tsend[3, 0, stats, :]], axis=0))
             combine_rows(parts, last * GROUP + c * PIECE, PIECE, picks(PIECE, c * PIECE))
 
         def p_wait(g):
@@ -298,6 +303,23 @@
             for d in far_first:
                 y_copy(b, g0, ng, d).start()
             y_out[3, sl, :] = ysend[me, sl, :]
+
+        def yl_copy(c, d):
+            return pltpu.make_async_remote_copy(
+                src_ref=ylsend.at[peers[d], c], dst_ref=yl_out.at[d, c], send_sem=yls_sem.at[d],
+                recv_sem=ylr_sem.at[c], device_id=(bx, peers[d]), device_id_type=MESH)
+
+        def project_piece(c):
+            r0 = last * GROUP + c * PIECE
+            lhs = attn[r0:r0 + PIECE, :].astype(jnp.bfloat16)
+            for side, near in ((1 - chip, False), (chip, True)):
+                col = pl.multiple_of(side * 2 * q_cols, 2 * q_cols)
+                yp = jnp.dot(lhs, wo[:, pl.ds(col, 2 * q_cols)], preferred_element_type=jnp.float32)
+                for k in range(2):
+                    ylsend[side * 2 + k, c] = yp[:, k * q_cols:(k + 1) * q_cols]
+                for d in ((0,) if near else (1, 2)):
+                    yl_copy(c, d).start()
+            yl_out[3, c] = ylsend[me, c]
 
         def finish(b, g0, ng):
             sl = pl.ds(g0 * GROUP, ng * GROUP)
@@ -357,23 +379,25 @@
                 oacc[rs, :] = weighted(last, r, wts[rs, :], 0, seq)
             send_piece(c, ml)
         done = max(g0 + ng for g0, ng in Y_BATCHES.values())
-        for g in (pre - 2, pre - 1):
+        for g in range(pre - 2, last):
             p_wait(g)
             combine(g)
-        project(done, pre - done)
-        p_wait(pre)
-        combine(pre)
-        project(pre, 1)
+            project(done, g + 1 - done)
+            done = g + 1
         for c in range(n_pieces):
             combine_piece(c)
-        project(last, 1)
+            project_piece(c)
         for b in y_batches:
             finish(*b)
+        for c in range(n_pieces):
+            pltpu.make_async_copy(yl_out.at[0:3, c], yl_out.at[0:3, c], ylr_sem.at[c]).wait()
         for d in range(3):
             pltpu.make_async_copy(qown, qown, qs_sem.at[d]).wait()
             pltpu.make_async_copy(psend.at[d], psend.at[d], ps_sem.at[d]).wait()
-            pltpu.make_async_copy(tsend.at[d], tsend.at[d], ts_sem.at[d]).wait()
+            for c in range(n_pieces):
+                t_copy(c, d).wait_send()
             pltpu.make_async_copy(ysend.at[d], ysend.at[d], ys_sem.at[d]).wait()
+            pltpu.make_async_copy(ylsend.at[d], ylsend.at[d], yls_sem.at[d]).wait()
 
     f32, bf16 = jnp.float32, jnp.bfloat16
     dma = pltpu.SemaphoreType.DMA
@@ -390,15 +414,19 @@
         pltpu.VMEM((hd, seq), bf16),
         pltpu.VMEM((4, last, prow + 8, hd), f32), pltpu.VMEM((last, 3, prow + 8, hd), f32),
         pltpu.VMEM((4, n_pieces, piece_rows + 8, hd), f32), pltpu.VMEM((n_pieces, 3, piece_rows + 8, hd), f32),
-        pltpu.VMEM((rows, q_cols), f32), pltpu.VMEM((4, rows, q_cols), f32),
+        pltpu.VMEM((rows, q_cols), f32), pltpu.VMEM((4, last * GROUP, q_cols), f32),
+        pltpu.VMEM((4, n_pieces, PIECE, q_cols), f32),
         dma((6,)), dma((RING,)), dma((RING,)), dma((n_pieces,)), dma((3,)), dma((n_groups,)),
-        dma((3,)), dma((last,)), dma((3,)), dma((n_pieces,)), dma((3,)), dma((n_b,)),
+        dma((3,)), dma((last,)), dma((3, n_pieces)), dma((n_pieces,)), dma((3,)), dma((n_pieces,)), dma((3,)), dma((n_b,)),
     ]
     return kernel, scratch
 
 
-def store_kernel(y_ref, k_ref, v_ref, yo_ref, ko_ref, vo_ref, y16, sem):
-    y16[...] = (y_ref[3] + y_ref[0] + y_ref[1] + y_ref[2]).astype(y16.dtype)
+def store_kernel(y_ref, yl_ref, k_ref, v_ref, yo_ref, ko_ref, vo_ref, y16, sem):
+    most = y_ref.shape[1]
+    y16[:most, :] = (y_ref[3] + y_ref[0] + y_ref[1] + y_ref[2]).astype(y16.dtype)
+    tail = [yl_ref[3, c] + yl_ref[0, c] + yl_ref[1, c] + yl_ref[2, c] for c in range(yl_ref.shape[1])]
+    y16[most:, :] = jnp.concatenate(tail, axis=0).astype(y16.dtype)
     writes = [pltpu.make_async_copy(a, b, sem.at[i])
               for i, (a, b) in enumerate(((y16, yo_ref), (k_ref, ko_ref), (v_ref, vo_ref)))]
     for w in writes:
@@ -422,10 +450,11 @@
                 jax.ShapeDtypeStruct((rows, hd), jnp.bfloat16))
         raw = pl.pallas_call(
             kernel,
-            out_shape=tuple(pltpu.VMEM(sh, dt) for sh, dt in (((4, rows, q_cols), jnp.float32),
+            out_shape=tuple(pltpu.VMEM(sh, dt) for sh, dt in (((4, rows - GROUP, q_cols), jnp.float32),
+                                                              ((4, GROUP // PIECE, PIECE, q_cols), jnp.float32),
                                                               ((rows, hd), jnp.bfloat16), ((rows, hd), jnp.bfloat16))),
             in_specs=[any_spec] * 8,
-            out_specs=(vmem_spec,) * 3,
+            out_specs=(vmem_spec,) * 4,
             scratch_shapes=scratch,
             compiler_params=pltpu.CompilerParams(
                 collective_id=0, has_side_effects=True, vmem_limit_bytes=66300000),
@@ -434,7 +463,7 @@
         return pl.pallas_call(
             store_kernel,
             out_shape=outs,
-            in_specs=[vmem_spec] * 3,
+            in_specs=[vmem_spec] * 4,
             out_specs=(any_spec,) * 3,
             scratch_shapes=[pltpu.VMEM(outs[0].shape, outs[0].dtype), pltpu.SemaphoreType.DMA((3,))],
             name="store_outputs",

time: 33.7 us -> 33.7 us (level)
  no operation moved by 1% of the time
where the time goes in v1:
time: 33.7 us; the launch traced here: 33.6 us
  Pallas kernels  32.8 us (97%)
  between operations  0.8 us (2%)
    pallas_call x1, Pallas kernels, local_step(): pl.pallas_call(kernel, out_shape=tuple((pltpu.VMEM(sh, dt) for sh, dt in...  32.1 us
    pallas_call x1, Pallas kernels, local_step(): pl.pallas_call(store_kernel, out_shape=outs, in_specs=[vmem_spec] * 4, ou...  0.69 us

profile of v1, /device:TPU:0, one launch (start us, length us, event | category | flops | bytes accessed | tf_op | source)
XLA Modules:
  0.0 33.6 jit_solution(11682848494532108793)
XLA Ops:
  0.6 32.1 %mqa_decode.1 = (f32[4,56,512]{2,1,0:T(8,128)S(1)}, f32[4,2,4,512]{3,2,1,0:T(4,128)S(1)}, bf16[64,128]{1,0:T(8,128)(2,1)S(1)}, bf16[64,128]{1,0:T(8,128)(2,1)S(1)}) custom-call(bf16[64,2048]{1,0:T(8,128)(2,1)} %hid_hbm.1, bf16[2048,512]{1,0:T(8,128)(2,1)} %wq_hbm.1, bf16[2048,128]{1,0:T(8,128)(2,1)} %wk_hbm.1, bf16[2048,128]{1,0:T(8,128)(2,1)} %wv_hbm.1, ...), custom_call_target="tpu_custom_call" | custom-call | tf_op jit(solution)/shard_map/mqa_decode/pallas_call | solution.py:451
  32.7 0.7 %store_outputs.1 = (bf16[64,512]{1,0:T(8,128)(2,1)}, bf16[64,128]{1,0:T(8,128)(2,1)}, bf16[64,128]{1,0:T(8,128)(2,1)}) custom-call(f32[4,56,512]{2,1,0:T(8,128)S(1)} %get-tuple-element.7.y_ref, f32[4,2,4,512]{3,2,1,0:T(4,128)S(1)} %get-tuple-element.8.yl_ref, bf16[64,128]{1,0:T(8,128)(2,1)S(1)} %get-tuple-element.9.k_ref, ...), custom_call_target="tpu_custom_call" | custom-call | tf_op jit(solution)/shard_map/store_outputs/pallas_call | solution.py:463
